TPU v7x, 512 devices: a whole 4x8x8 slice. The times are simulated.
512 devices in a mesh: orb: 4 (over x), gx: 8 (over y), gyz: 16 (over z, core).
Axes of the slice: x: 4, y: 8, z: 8, core: 2. Of those that a mesh axis runs over, the one named last changes fastest.
Arguments:
- orbitals: float32 [2, 12, 128, 128, 128], P(None, 'orb', 'gx', 'gyz'), parts along dimension 1, may hold values from -12 to 12
- potential: float32 [128, 128, 128], P('gx', 'gyz'), may hold values from -8 to 60
Outputs:
- evolved: float32 [2, 12, 128, 128, 128], P(None, 'orb', 'gx', 'gyz'), parts along dimension 1
- residual: float32 [2, 12, 128, 128, 128], P(None, 'orb', 'gx', 'gyz'), parts along dimension 1
There are 4 independent parts, one for each index of `orb`. A program takes and returns all parts, laid end to end along the dimension named above; an argument that names none is the same for every part. Nothing has to cross between parts.
All inputs are finite; a program needn't handle non-finite values.
Results may differ from a plain program's by a relative error of at most 0.0003.
Values sent between devices are 32-bit elements; how exact they have to be, the bound alone decides.
A program may use at most 64 MiB of HBM per device.

v0:
```python
import jax
import jax.numpy as jnp
from jax import lax
from jax.sharding import Mesh
from jax.sharding import PartitionSpec as P

ITERS = 4
GX_GYZ = ("gx", "gyz_0", "gyz_1")
GYZ = ("gyz_0", "gyz_1")
SPACING = 0.25
HALF_STEP = 0.05
COEFF_NEAR = 4.0 / 3.0
COEFF_FAR = -1.0 / 12.0
COEFF_SELF = -2.5


def padded_2(array, sides, width):
    edges = {}
    for axis, dim in sides:
        size, length = (lax.axis_size(axis), array.shape[dim])
        up = [(i, (i + 1) % size) for i in range(size - 1)]
        last = lax.slice_in_dim(array, length - width, length, axis=dim)
        leading = lax.slice_in_dim(array, 0, width, axis=dim)
        edges[dim] = (
            lax.ppermute(last, axis, up),
            lax.ppermute(leading, axis, [(b, a) for a, b in up]),
        )
    done = []
    for _, dim in sides:
        low, high = edges[dim]
        around = [(width, width) if d in done else (0, 0) for d in range(array.ndim)]
        array = jnp.concatenate([jnp.pad(low, around), array, jnp.pad(high, around)], axis=dim)
        done.append(dim)
    return array


def by_axis(array, axes):
    for axis in axes:
        array = lax.psum(array, axis)
    return array


def laplace_apply(padded, potential):
    extent = (padded.shape[2] - 4, padded.shape[3] - 4, padded.shape[4] - 4)

    def window(shift_x, shift_y, shift_z):
        return padded[
            :,
            :,
            2 + shift_x : 2 + shift_x + extent[0],
            2 + shift_y : 2 + shift_y + extent[1],
            2 + shift_z : 2 + shift_z + extent[2],
        ]

    center = window(0, 0, 0)
    summed = 3.0 * COEFF_SELF * center
    for offset, weight in ((1, COEFF_NEAR), (2, COEFF_FAR)):
        summed = summed + weight * (
            window(offset, 0, 0)
            + window(-offset, 0, 0)
            + window(0, offset, 0)
            + window(0, -offset, 0)
            + window(0, 0, offset)
            + window(0, 0, -offset)
        )
    return -0.5 / SPACING**2 * summed + potential * center


def pad_depth(vector):
    return jnp.pad(vector, ((0, 0), (0, 0), (0, 0), (0, 0), (2, 2)))


def system(vector, applied):
    return jnp.stack([vector[0] - HALF_STEP * applied[1], vector[1] + HALF_STEP * applied[0]])


def precondition(vector, potential):
    diagonal = HALF_STEP * (3.75 / SPACING**2 + potential)
    divisor = 1.0 + diagonal * diagonal
    return jnp.stack(
        [(vector[0] + diagonal * vector[1]) / divisor, (vector[1] - diagonal * vector[0]) / divisor]
    )


def braket(left, right):
    real_part = jnp.sum(left[0] * right[0] + left[1] * right[1], axis=(1, 2, 3))
    imag_part = jnp.sum(left[0] * right[1] - left[1] * right[0], axis=(1, 2, 3))
    return (real_part, imag_part)


def times_complex(first, second):
    return (
        first[0] * second[0] - first[1] * second[1],
        first[0] * second[1] + first[1] * second[0],
    )


def divide_complex(first, second):
    modulus = second[0] * second[0] + second[1] * second[1]
    return (
        (first[0] * second[0] + first[1] * second[1]) / modulus,
        (first[1] * second[0] - first[0] * second[1]) / modulus,
    )


def scale_complex(coeff, vector):
    real_coef = coeff[0][:, None, None, None]
    imag_coef = coeff[1][:, None, None, None]
    return jnp.stack(
        [
            real_coef * vector[0] - imag_coef * vector[1],
            real_coef * vector[1] + imag_coef * vector[0],
        ]
    )


def shards(orbitals, potential):

    def apply_shallow(vector):
        padded = padded_2(vector, (("gx", 2), (GYZ, 3)), 2)
        return laplace_apply(pad_depth(padded), potential)

    h_orbitals = apply_shallow(orbitals)
    residual = jnp.stack([2.0 * HALF_STEP * h_orbitals[1], -2.0 * HALF_STEP * h_orbitals[0]])
    evolved = orbitals
    shadow = residual
    direction = residual
    rho_now = jax.tree.map(lambda part: by_axis(part, GX_GYZ), braket(shadow, residual))
    for iteration in range(ITERS):
        dir_hat = precondition(direction, potential)
        image = system(dir_hat, apply_shallow(dir_hat))
        alpha_step = divide_complex(
            rho_now, jax.tree.map(lambda part: by_axis(part, GX_GYZ), braket(shadow, image))
        )
        half_step = residual - scale_complex(alpha_step, image)
        half_hat = precondition(half_step, potential)
        second = system(half_hat, apply_shallow(half_hat))
        cross_local = braket(second, half_step)
        norm_local = jnp.sum(second * second, axis=(0, 2, 3, 4))
        shadow_half = braket(shadow, half_step)
        shadow_second = braket(shadow, second)
        summed = (
            by_axis(cross_local[0], GX_GYZ),
            by_axis(cross_local[1], GX_GYZ),
            by_axis(norm_local, GX_GYZ),
            by_axis(shadow_half[0], GX_GYZ),
            by_axis(shadow_half[1], GX_GYZ),
            by_axis(shadow_second[0], GX_GYZ),
            by_axis(shadow_second[1], GX_GYZ),
        )
        cross_real, cross_imag, norm_second = (summed[0], summed[1], summed[2])
        omega_step = (cross_real / norm_second, cross_imag / norm_second)
        evolved = evolved + scale_complex(alpha_step, dir_hat) + scale_complex(omega_step, half_hat)
        residual = half_step - scale_complex(omega_step, second)
        if iteration + 1 < ITERS:
            along_second = times_complex(omega_step, (summed[5], summed[6]))
            rho_next = (summed[3] - along_second[0], summed[4] - along_second[1])
            beta_step = times_complex(
                divide_complex(rho_next, rho_now), divide_complex(alpha_step, omega_step)
            )
            direction = residual + scale_complex(
                beta_step, direction - scale_complex(omega_step, image)
            )
            rho_now = rho_next
    return (evolved, residual)


def solution(mesh):
    finer = Mesh(
        mesh.devices.reshape(mesh.shape["orb"], mesh.shape["gx"], 8, 2),
        ("orb", "gx", "gyz_0", "gyz_1"),
    )
    return jax.shard_map(
        shards,
        mesh=finer,
        in_specs=(P(None, "orb", "gx", GYZ, None), P("gx", GYZ, None)),
        out_specs=(P(None, "orb", "gx", GYZ, None), P(None, "orb", "gx", GYZ, None)),
        check_vma=False,
    )
```

profile of v0, /device:TPU:1, one launch (start us, length us, event | category | flops | bytes accessed | tf_op | source)
XLA Modules:
  0.0 460.2 jit_solution(8637743133134373983)
XLA Ops:
  2.8 4.6 %collective-permute-start.1 = (f32[2,3,2,8,128]{4,3,2,1,0:T(8,128)S(1)}, f32[2,3,2,8,128]{4,3,2,1,0:T(8,128)S(1)}, u32[]{:S(2)}, u32[]{:S(2)}) collective-permute-start(f32[2,3,2,8,128]{4,3,2,1,0:T(8,128)S(1)} %get-tuple-element.312), channel_id=1, source_target_pairs={{0,16},{16,32},{32,48},{48,64},{64,80},{80,96},{96,112},{1,17},{17... | collective-permute-start | bytes 147464 | tf_op jit(solution)/shard_map/ppermute | solution.py:25
  8.6 5.3 %collective-permute-start.3 = (f32[2,3,16,2,128]{4,3,2,1,0:T(2,128)S(1)}, f32[2,3,16,2,128]{4,3,2,1,0:T(2,128)S(1)}, u32[]{:S(2)}, u32[]{:S(2)}) collective-permute-start(f32[2,3,16,2,128]{4,3,2,1,0:T(2,128)S(1)} %get-tuple-element.309), channel_id=1, source_target_pairs={{0,1},{1,2},{2,3},{3,4},{4,5},{5,6},{6,7},{7,8},{8,9},{9,10},{10,1... | collective-permute-start | bytes 294920 | tf_op jit(solution)/shard_map/ppermute | solution.py:25
  13.9 4.7 %collective-permute-start.2 = (f32[2,3,16,2,128]{4,3,2,1,0:T(2,128)S(1)}, f32[2,3,16,2,128]{4,3,2,1,0:T(2,128)S(1)}, u32[]{:S(2)}, u32[]{:S(2)}) collective-permute-start(f32[2,3,16,2,128]{4,3,2,1,0:T(2,128)S(1)} %get-tuple-element.310), channel_id=1, source_target_pairs={{1,0},{2,1},{3,2},{4,3},{5,4},{6,5},{7,6},{8,7},{9,8},{10,9},{11,1... | collective-permute-start | bytes 294920 | tf_op jit(solution)/shard_map/ppermute | solution.py:26
  22.6 2.3 collective-permute-start.5
  26.3 2.1 collective-permute-start.7
  28.4 2.2 collective-permute-start.6
  30.8 4.1 collective-permute-done.6
  37.0 14.2 %all-reduce.42 = (f32[3]{0:T(128)S(1)}, f32[3]{0:T(128)S(1)}, f32[3]{0:T(128)S(1)}, f32[3]{0:T(128)S(1)}) all-reduce(f32[3]{0:T(128)S(1)} %get-tuple-element.43, f32[3]{0:T(128)S(1)} %get-tuple-element.3, f32[3]{0:T(128)S(1)} %get-tuple-element.42, f32[3]{0:T(128)S(1)} %get-tuple-element.2), channel_id=1, replica_groups=mesh['orb'=4,'gx'=8,'gyz_0'=8,'gyz_1'=2] {'gx'}, use_global_device_ids=true, to_apply=%region_1.2 | all-reduce | flops 12 | bytes 96 | tf_op jit(solution)/shard_map/psum | solution.py:39
  51.3 17.8 %all-reduce.34 = (f32[3]{0:T(128)S(1)}, f32[3]{0:T(128)S(1)}, f32[3]{0:T(128)S(1)}, f32[3]{0:T(128)S(1)}) all-reduce(f32[3]{0:T(128)S(1)} %get-tuple-element.108, f32[3]{0:T(128)S(1)} %get-tuple-element.109, f32[3]{0:T(128)S(1)} %get-tuple-element.110, ...), channel_id=1, replica_groups=mesh['orb'=4,'gx'=8,'gyz_0'=8,'gyz_1'=2] {'gyz_0'}, use_global_device_ids=true, to_apply=%region_2.3 | all-reduce | flops 12 | bytes 96 | tf_op jit(solution)/shard_map/psum | solution.py:39
  69.1 8.8 %all-reduce.50 = (f32[3]{0:T(128)S(1)}, f32[3]{0:T(128)S(1)}, f32[3]{0:T(128)S(1)}, f32[3]{0:T(128)S(1)}) all-reduce(f32[3]{0:T(128)S(1)} %get-tuple-element.74, f32[3]{0:T(128)S(1)} %get-tuple-element.75, f32[3]{0:T(128)S(1)} %get-tuple-element.76, ...), channel_id=1, replica_groups=mesh['orb'=4,'gx'=8,'gyz_0'=8,'gyz_1'=2] {'gyz_1'}, use_global_device_ids=true, to_apply=%region_3.4 | all-reduce | flops 12 | bytes 96 | tf_op jit(solution)/shard_map/psum | solution.py:39
  79.0 3.0 collective-permute-start.9
  83.3 1.9 collective-permute-start.11
  85.2 2.4 collective-permute-start.10
  87.8 3.4 collective-permute-done.10
  93.6 14.2 %all-reduce.41 = (f32[3]{0:T(128)S(1)}, f32[3]{0:T(128)S(1)}, f32[3]{0:T(128)S(1)}, f32[3]{0:T(128)S(1)}, f32[3]{0:T(128)S(1)}, /*index=5*/f32[3]{0:T(128)S(1)}, f32[3]{0:T(128)S(1)}) all-reduce(f32[3]{0:T(128)S(1)} %get-tuple-element.40, f32[3]{0:T(128)S(1)} %fusion.80, ...), channel_id=1, replica_groups=mesh['orb'=4,'gx'=8,'gyz_0'=8,'gyz_1'=2] {'gx'}, use_global_device_ids=true, to_apply=%region_25.26 | all-reduce | flops 21 | bytes 168 | tf_op jit(solution)/shard_map/psum | solution.py:39
  107.8 13.0 %all-reduce.33 = (f32[3]{0:T(128)S(1)}, f32[3]{0:T(128)S(1)}, f32[3]{0:T(128)S(1)}, f32[3]{0:T(128)S(1)}, f32[3]{0:T(128)S(1)}, /*index=5*/f32[3]{0:T(128)S(1)}, f32[3]{0:T(128)S(1)}) all-reduce(f32[3]{0:T(128)S(1)} %get-tuple-element.101, ...), channel_id=1, replica_groups=mesh['orb'=4,'gx'=8,'gyz_0'=8,'gyz_1'=2] {'gyz_0'}, use_global_device_ids=true, to_apply=%region_26.27 | all-reduce | flops 21 | bytes 168 | tf_op jit(solution)/shard_map/psum | solution.py:39
  120.8 8.4 %all-reduce.49 = (f32[3]{0:T(128)S(1)}, f32[3]{0:T(128)S(1)}, f32[3]{0:T(128)S(1)}, f32[3]{0:T(128)S(1)}, f32[3]{0:T(128)S(1)}, /*index=5*/f32[3]{0:T(128)S(1)}, f32[3]{0:T(128)S(1)}) all-reduce(f32[3]{0:T(128)S(1)} %get-tuple-element.67, f32[3]{0:T(128)S(1)} %get-tuple-element.68, ...), channel_id=1, replica_groups=mesh['orb'=4,'gx'=8,'gyz_0'=8,'gyz_1'=2] {'gyz_1'}, use_global_device_ids=true, to_apply=%region_27.28 | all-reduce | flops 21 | bytes 168 | tf_op jit(solution)/shard_map/psum | solution.py:39
  130.6 2.0 collective-permute-start.13
  134.1 2.2 collective-permute-start.15
  136.3 2.1 collective-permute-start.14
  138.6 3.6 collective-permute-done.14
  144.3 14.2 %all-reduce.40 = (f32[3]{0:T(128)S(1)}, f32[3]{0:T(128)S(1)}) all-reduce(f32[3]{0:T(128)S(1)} %get-tuple-element.23, f32[3]{0:T(128)S(1)} %get-tuple-element.22), channel_id=1, replica_groups=mesh['orb'=4,'gx'=8,'gyz_0'=8,'gyz_1'=2] {'gx'}, use_global_device_ids=true, to_apply=%region_49.50 | all-reduce | flops 6 | bytes 48 | tf_op jit(solution)/shard_map/psum | solution.py:39
  158.5 14.3 %all-reduce.32 = (f32[3]{0:T(128)S(1)}, f32[3]{0:T(128)S(1)}) all-reduce(f32[3]{0:T(128)S(1)} %get-tuple-element.99, f32[3]{0:T(128)S(1)} %get-tuple-element.100), channel_id=1, replica_groups=mesh['orb'=4,'gx'=8,'gyz_0'=8,'gyz_1'=2] {'gyz_0'}, use_global_device_ids=true, to_apply=%region_50.51 | all-reduce | flops 6 | bytes 48 | tf_op jit(solution)/shard_map/psum | solution.py:39
  172.8 7.4 %all-reduce.48 = (f32[3]{0:T(128)S(1)}, f32[3]{0:T(128)S(1)}) all-reduce(f32[3]{0:T(128)S(1)} %get-tuple-element.65, f32[3]{0:T(128)S(1)} %get-tuple-element.66), channel_id=1, replica_groups=mesh['orb'=4,'gx'=8,'gyz_0'=8,'gyz_1'=2] {'gyz_1'}, use_global_device_ids=true, to_apply=%region_51.52 | all-reduce | flops 6 | bytes 48 | tf_op jit(solution)/shard_map/psum | solution.py:39
  181.9 2.0 collective-permute-start.17
  185.2 2.9 collective-permute-start.19
  188.1 1.9 collective-permute-start.18
  190.2 3.9 collective-permute-done.18
  197.1 14.7 %all-reduce.39 = (f32[3]{0:T(128)S(1)}, f32[3]{0:T(128)S(1)}, f32[3]{0:T(128)S(1)}, f32[3]{0:T(128)S(1)}, f32[3]{0:T(128)S(1)}, /*index=5*/f32[3]{0:T(128)S(1)}, f32[3]{0:T(128)S(1)}) all-reduce(f32[3]{0:T(128)} %get-tuple-element.36, f32[3]{0:T(128)S(1)} %fusion.81, ...), channel_id=1, replica_groups=mesh['orb'=4,'gx'=8,'gyz_0'=8,'gyz_1'=2] {'gx'}, use_global_device_ids=true, to_apply=%region_61.62 | all-reduce | flops 21 | bytes 168 | tf_op jit(solution)/shard_map/psum | solution.py:39
  211.7 12.8 %all-reduce.31 = (f32[3]{0:T(128)S(1)}, f32[3]{0:T(128)S(1)}, f32[3]{0:T(128)S(1)}, f32[3]{0:T(128)S(1)}, f32[3]{0:T(128)S(1)}, /*index=5*/f32[3]{0:T(128)S(1)}, f32[3]{0:T(128)S(1)}) all-reduce(f32[3]{0:T(128)S(1)} %get-tuple-element.92, f32[3]{0:T(128)S(1)} %get-tuple-element.93, ...), channel_id=1, replica_groups=mesh['orb'=4,'gx'=8,'gyz_0'=8,'gyz_1'=2] {'gyz_0'}, use_global_device_ids=true, to_apply=%region_62.63 | all-reduce | flops 21 | bytes 168 | tf_op jit(solution)/shard_map/psum | solution.py:39
  224.6 8.4 %all-reduce.47 = (f32[3]{0:T(128)S(1)}, f32[3]{0:T(128)S(1)}, f32[3]{0:T(128)S(1)}, f32[3]{0:T(128)S(1)}, f32[3]{0:T(128)S(1)}, /*index=5*/f32[3]{0:T(128)S(1)}, f32[3]{0:T(128)S(1)}) all-reduce(f32[3]{0:T(128)S(1)} %get-tuple-element.58, f32[3]{0:T(128)S(1)} %get-tuple-element.59, ...), channel_id=1, replica_groups=mesh['orb'=4,'gx'=8,'gyz_0'=8,'gyz_1'=2] {'gyz_1'}, use_global_device_ids=true, to_apply=%region_63.64 | all-reduce | flops 21 | bytes 168 | tf_op jit(solution)/shard_map/psum | solution.py:39
  233.7 2.1 multiply_subtract_fusion.12
  237.8 2.0 collective-permute-start.21
  241.2 2.2 collective-permute-start.23
  243.4 2.1 collective-permute-start.22
  245.7 3.7 collective-permute-done.22
  252.1 14.2 %all-reduce.38 = (f32[3]{0:T(128)S(1)}, f32[3]{0:T(128)S(1)}) all-reduce(f32[3]{0:T(128)S(1)} %get-tuple-element.15, f32[3]{0:T(128)S(1)} %get-tuple-element.14), channel_id=1, replica_groups=mesh['orb'=4,'gx'=8,'gyz_0'=8,'gyz_1'=2] {'gx'}, use_global_device_ids=true, to_apply=%region_85.86 | all-reduce | flops 6 | bytes 48 | tf_op jit(solution)/shard_map/psum | solution.py:39
  266.4 14.1 %all-reduce.30 = (f32[3]{0:T(128)S(1)}, f32[3]{0:T(128)S(1)}) all-reduce(f32[3]{0:T(128)S(1)} %get-tuple-element.90, f32[3]{0:T(128)S(1)} %get-tuple-element.91), channel_id=1, replica_groups=mesh['orb'=4,'gx'=8,'gyz_0'=8,'gyz_1'=2] {'gyz_0'}, use_global_device_ids=true, to_apply=%region_86.87 | all-reduce | flops 6 | bytes 48 | tf_op jit(solution)/shard_map/psum | solution.py:39
  280.4 7.5 %all-reduce.46 = (f32[3]{0:T(128)S(1)}, f32[3]{0:T(128)S(1)}) all-reduce(f32[3]{0:T(128)S(1)} %get-tuple-element.56, f32[3]{0:T(128)S(1)} %get-tuple-element.57), channel_id=1, replica_groups=mesh['orb'=4,'gx'=8,'gyz_0'=8,'gyz_1'=2] {'gyz_1'}, use_global_device_ids=true, to_apply=%region_87.88 | all-reduce | flops 6 | bytes 48 | tf_op jit(solution)/shard_map/psum | solution.py:39
  287.9 1.9 multiply_subtract_fusion.8
  290.8 2.0 collective-permute-start.25
  294.1 2.9 collective-permute-start.27
  297.0 1.9 collective-permute-start.26
  299.1 3.9 collective-permute-done.26
  306.6 15.2 %all-reduce.37 = (f32[3]{0:T(128)}, f32[3]{0:T(128)}, f32[3]{0:T(128)}, f32[3]{0:T(128)}, f32[3]{0:T(128)}, /*index=5*/f32[3]{0:T(128)}, f32[3]{0:T(128)}) all-reduce(f32[3]{0:T(128)} %get-tuple-element.32, f32[3]{0:T(128)} %fusion.82, f32[3]{0:T(128)} %get-tuple-element.33, ...), channel_id=1, replica_groups=mesh['orb'=4,'gx'=8,'gyz_0'=8,'gyz_1'=2] {'gx'}, use_global_device_ids=true, to_apply=%region_97.98 | all-reduce | flops 21 | bytes 168 | tf_op jit(solution)/shard_map/psum | solution.py:39
  321.8 13.9 %all-reduce.29 = (f32[3]{0:T(128)}, f32[3]{0:T(128)}, f32[3]{0:T(128)}, f32[3]{0:T(128)}, f32[3]{0:T(128)}, /*index=5*/f32[3]{0:T(128)}, f32[3]{0:T(128)}) all-reduce(f32[3]{0:T(128)} %get-tuple-element.83, f32[3]{0:T(128)} %get-tuple-element.84, ...), channel_id=1, replica_groups=mesh['orb'=4,'gx'=8,'gyz_0'=8,'gyz_1'=2] {'gyz_0'}, use_global_device_ids=true, to_apply=%region_98.99 | all-reduce | flops 21 | bytes 168 | tf_op jit(solution)/shard_map/psum | solution.py:39
  335.7 8.8 %all-reduce.45 = (f32[3]{0:T(128)}, f32[3]{0:T(128)}, f32[3]{0:T(128)}, f32[3]{0:T(128)}, f32[3]{0:T(128)}, /*index=5*/f32[3]{0:T(128)}, f32[3]{0:T(128)}) all-reduce(f32[3]{0:T(128)} %get-tuple-element.49, f32[3]{0:T(128)} %get-tuple-element.50, ...), channel_id=1, replica_groups=mesh['orb'=4,'gx'=8,'gyz_0'=8,'gyz_1'=2] {'gyz_1'}, use_global_device_ids=true, to_apply=%region_99.100 | all-reduce | flops 21 | bytes 168 | tf_op jit(solution)/shard_map/psum | solution.py:39
  345.8 2.2 multiply_subtract_fusion.6
  349.4 2.0 collective-permute-start.29
  352.8 2.2 collective-permute-start.31
  355.0 2.3 collective-permute-start.30
  357.5 3.5 collective-permute-done.30
  363.5 14.2 %all-reduce.36 = (f32[3]{0:T(128)S(1)}, f32[3]{0:T(128)S(1)}) all-reduce(f32[3]{0:T(128)S(1)} %get-tuple-element.7, f32[3]{0:T(128)S(1)} %get-tuple-element.6), channel_id=1, replica_groups=mesh['orb'=4,'gx'=8,'gyz_0'=8,'gyz_1'=2] {'gx'}, use_global_device_ids=true, to_apply=%region_121.122 | all-reduce | flops 6 | bytes 48 | tf_op jit(solution)/shard_map/psum | solution.py:39
  377.7 14.1 %all-reduce.28 = (f32[3]{0:T(128)S(1)}, f32[3]{0:T(128)S(1)}) all-reduce(f32[3]{0:T(128)S(1)} %get-tuple-element.81, f32[3]{0:T(128)S(1)} %get-tuple-element.82), channel_id=1, replica_groups=mesh['orb'=4,'gx'=8,'gyz_0'=8,'gyz_1'=2] {'gyz_0'}, use_global_device_ids=true, to_apply=%region_122.123 | all-reduce | flops 6 | bytes 48 | tf_op jit(solution)/shard_map/psum | solution.py:39
  391.8 7.5 %all-reduce.44 = (f32[3]{0:T(128)S(1)}, f32[3]{0:T(128)S(1)}) all-reduce(f32[3]{0:T(128)S(1)} %get-tuple-element.47, f32[3]{0:T(128)S(1)} %get-tuple-element.48), channel_id=1, replica_groups=mesh['orb'=4,'gx'=8,'gyz_0'=8,'gyz_1'=2] {'gyz_1'}, use_global_device_ids=true, to_apply=%region_123.124 | all-reduce | flops 6 | bytes 48 | tf_op jit(solution)/shard_map/psum | solution.py:39
  399.3 2.0 multiply_subtract_fusion.2
  403.3 2.0 collective-permute-start.33
  406.7 2.9 collective-permute-start.35
  409.6 1.9 collective-permute-start.34
  411.7 3.9 collective-permute-done.34
  418.4 15.1 %all-reduce.35 = (f32[3]{0:T(128)S(1)}, f32[3]{0:T(128)}, f32[3]{0:T(128)}) all-reduce(f32[3]{0:T(128)S(1)} %get-tuple-element.5, f32[3]{0:T(128)S(1)} %fusion.83, f32[3]{0:T(128)S(1)} %get-tuple-element.4), channel_id=1, replica_groups=mesh['orb'=4,'gx'=8,'gyz_0'=8,'gyz_1'=2] {'gx'}, use_global_device_ids=true, to_apply=%region_133.134 | all-reduce | flops 9 | bytes 72 | tf_op jit(solution)/shard_map/psum | solution.py:39
  433.5 13.9 %all-reduce.27 = (f32[3]{0:T(128)}, f32[3]{0:T(128)}, f32[3]{0:T(128)}) all-reduce(f32[3]{0:T(128)S(1)} %get-tuple-element.78, f32[3]{0:T(128)} %get-tuple-element.79, f32[3]{0:T(128)} %get-tuple-element.80), channel_id=1, replica_groups=mesh['orb'=4,'gx'=8,'gyz_0'=8,'gyz_1'=2] {'gyz_0'}, use_global_device_ids=true, to_apply=%region_134.135 | all-reduce | flops 9 | bytes 72 | tf_op jit(solution)/shard_map/psum | solution.py:39
  447.4 8.2 %all-reduce.43 = (f32[3]{0:T(128)S(1)}, f32[3]{0:T(128)S(1)}, f32[3]{0:T(128)S(1)}) all-reduce(f32[3]{0:T(128)} %get-tuple-element.44, f32[3]{0:T(128)} %get-tuple-element.45, f32[3]{0:T(128)} %get-tuple-element.46), channel_id=1, replica_groups=mesh['orb'=4,'gx'=8,'gyz_0'=8,'gyz_1'=2] {'gyz_1'}, use_global_device_ids=true, to_apply=%region_135.136 | all-reduce | flops 9 | bytes 72 | tf_op jit(solution)/shard_map/psum | solution.py:39
  457.0 2.1 maximum_subtract_fusion.10
  (257 shorter events, 54.7 us)
Async XLA Ops:
  1.5 19.1 %collective-permute-start = (f32[2,3,2,8,128]{4,3,2,1,0:T(8,128)S(1)}, f32[2,3,2,8,128]{4,3,2,1,0:T(8,128)S(1)}, u32[]{:S(2)}, u32[]{:S(2)}) collective-permute-start(f32[2,3,2,8,128]{4,3,2,1,0:T(8,128)S(1)} %get-tuple-element.311), channel_id=1, source_target_pairs={{16,0},{32,16},{48,32},{64,48},{80,64},{96,80},{112,96},{17,1},{33... | collective-permute-start | bytes 147464 | tf_op jit(solution)/shard_map/ppermute | solution.py:26
  2.8 16.7 %collective-permute-start.1 = (f32[2,3,2,8,128]{4,3,2,1,0:T(8,128)S(1)}, f32[2,3,2,8,128]{4,3,2,1,0:T(8,128)S(1)}, u32[]{:S(2)}, u32[]{:S(2)}) collective-permute-start(f32[2,3,2,8,128]{4,3,2,1,0:T(8,128)S(1)} %get-tuple-element.312), channel_id=1, source_target_pairs={{0,16},{16,32},{32,48},{48,64},{64,80},{80,96},{96,112},{1,17},{17... | collective-permute-start | bytes 147464 | tf_op jit(solution)/shard_map/ppermute | solution.py:25
  8.6 12.0 %collective-permute-start.3 = (f32[2,3,16,2,128]{4,3,2,1,0:T(2,128)S(1)}, f32[2,3,16,2,128]{4,3,2,1,0:T(2,128)S(1)}, u32[]{:S(2)}, u32[]{:S(2)}) collective-permute-start(f32[2,3,16,2,128]{4,3,2,1,0:T(2,128)S(1)} %get-tuple-element.309), channel_id=1, source_target_pairs={{0,1},{1,2},{2,3},{3,4},{4,5},{5,6},{6,7},{7,8},{8,9},{9,10},{10,1... | collective-permute-start | bytes 294920 | tf_op jit(solution)/shard_map/ppermute | solution.py:25
  13.9 6.8 %collective-permute-start.2 = (f32[2,3,16,2,128]{4,3,2,1,0:T(2,128)S(1)}, f32[2,3,16,2,128]{4,3,2,1,0:T(2,128)S(1)}, u32[]{:S(2)}, u32[]{:S(2)}) collective-permute-start(f32[2,3,16,2,128]{4,3,2,1,0:T(2,128)S(1)} %get-tuple-element.310), channel_id=1, source_target_pairs={{1,0},{2,1},{3,2},{4,3},{5,4},{6,5},{7,6},{8,7},{9,8},{10,9},{11,1... | collective-permute-start | bytes 294920 | tf_op jit(solution)/shard_map/ppermute | solution.py:26
  20.6 1.3 copy-start
  22.6 8.1 %collective-permute-start.5 = (f32[2,3,2,8,128]{4,3,2,1,0:T(8,128)S(1)}, f32[2,3,2,8,128]{4,3,2,1,0:T(8,128)S(1)}, u32[]{:S(2)}, u32[]{:S(2)}) collective-permute-start(f32[2,3,2,8,128]{4,3,2,1,0:T(8,128)S(1)} %get-tuple-element.302), channel_id=1, source_target_pairs={{0,16},{16,32},{32,48},{48,64},{64,80},{80,96},{96,112},{1,17},{17... | collective-permute-start | bytes 147464 | tf_op jit(solution)/shard_map/ppermute | solution.py:25
  25.0 5.7 %collective-permute-start.4 = (f32[2,3,2,8,128]{4,3,2,1,0:T(8,128)S(1)}, f32[2,3,2,8,128]{4,3,2,1,0:T(8,128)S(1)}, u32[]{:S(2)}, u32[]{:S(2)}) collective-permute-start(f32[2,3,2,8,128]{4,3,2,1,0:T(8,128)S(1)} %get-tuple-element.303), channel_id=1, source_target_pairs={{16,0},{32,16},{48,32},{64,48},{80,64},{96,80},{112,96},{17,1},{33... | collective-permute-start | bytes 147464 | tf_op jit(solution)/shard_map/ppermute | solution.py:26
  26.3 4.4 collective-permute-start.7
  28.4 6.5 %collective-permute-start.6 = (f32[2,3,16,2,128]{4,3,2,1,0:T(2,128)S(1)}, f32[2,3,16,2,128]{4,3,2,1,0:T(2,128)S(1)}, u32[]{:S(2)}, u32[]{:S(2)}) collective-permute-start(f32[2,3,16,2,128]{4,3,2,1,0:T(2,128)S(1)} %get-tuple-element.305), channel_id=1, source_target_pairs={{1,0},{2,1},{3,2},{4,3},{5,4},{6,5},{7,6},{8,7},{9,8},{10,9},{11,1... | collective-permute-start | bytes 294920 | tf_op jit(solution)/shard_map/ppermute | solution.py:26
  79.0 8.7 %collective-permute-start.9 = (f32[2,3,2,8,128]{4,3,2,1,0:T(8,128)S(1)}, f32[2,3,2,8,128]{4,3,2,1,0:T(8,128)S(1)}, u32[]{:S(2)}, u32[]{:S(2)}) collective-permute-start(f32[2,3,2,8,128]{4,3,2,1,0:T(8,128)S(1)} %get-tuple-element.294), channel_id=1, source_target_pairs={{0,16},{16,32},{32,48},{48,64},{64,80},{80,96},{96,112},{1,17},{17... | collective-permute-start | bytes 147464 | tf_op jit(solution)/shard_map/ppermute | solution.py:25
  81.9 5.7 %collective-permute-start.8 = (f32[2,3,2,8,128]{4,3,2,1,0:T(8,128)S(1)}, f32[2,3,2,8,128]{4,3,2,1,0:T(8,128)S(1)}, u32[]{:S(2)}, u32[]{:S(2)}) collective-permute-start(f32[2,3,2,8,128]{4,3,2,1,0:T(8,128)S(1)} %get-tuple-element.295), channel_id=1, source_target_pairs={{16,0},{32,16},{48,32},{64,48},{80,64},{96,80},{112,96},{17,1},{33... | collective-permute-start | bytes 147464 | tf_op jit(solution)/shard_map/ppermute | solution.py:26
  83.3 4.4 collective-permute-start.11
  85.2 5.9 %collective-permute-start.10 = (f32[2,3,16,2,128]{4,3,2,1,0:T(2,128)S(1)}, f32[2,3,16,2,128]{4,3,2,1,0:T(2,128)S(1)}, u32[]{:S(2)}, u32[]{:S(2)}) collective-permute-start(f32[2,3,16,2,128]{4,3,2,1,0:T(2,128)S(1)} %get-tuple-element.297), channel_id=1, source_target_pairs={{1,0},{2,1},{3,2},{4,3},{5,4},{6,5},{7,6},{8,7},{9,8},{10,9},{11,1... | collective-permute-start | bytes 294920 | tf_op jit(solution)/shard_map/ppermute | solution.py:26
  129.3 50.9 %copy-start.42 = (f32[3]{0:T(128)}, f32[3]{0:T(128)S(1)}, u32[]{:S(2)}) copy-start(f32[3]{0:T(128)S(1)} %get-tuple-element.175) | copy-start | bytes 40
  129.3 50.9 %copy-start.43 = (f32[3]{0:T(128)}, f32[3]{0:T(128)S(1)}, u32[]{:S(2)}) copy-start(f32[3]{0:T(128)S(1)} %get-tuple-element.176) | copy-start | bytes 40
  130.4 3.6 copy-start.20
  130.5 3.6 copy-start.21
  130.6 7.8 %collective-permute-start.13 = (f32[2,3,2,8,128]{4,3,2,1,0:T(8,128)S(1)}, f32[2,3,2,8,128]{4,3,2,1,0:T(8,128)S(1)}, u32[]{:S(2)}, u32[]{:S(2)}) collective-permute-start(f32[2,3,2,8,128]{4,3,2,1,0:T(8,128)S(1)} %get-tuple-element.286), channel_id=1, source_target_pairs={{0,16},{16,32},{32,48},{48,64},{64,80},{80,96},{96,112},{1,17},{17... | collective-permute-start | bytes 147464 | tf_op jit(solution)/shard_map/ppermute | solution.py:25
  132.7 5.7 %collective-permute-start.12 = (f32[2,3,2,8,128]{4,3,2,1,0:T(8,128)S(1)}, f32[2,3,2,8,128]{4,3,2,1,0:T(8,128)S(1)}, u32[]{:S(2)}, u32[]{:S(2)}) collective-permute-start(f32[2,3,2,8,128]{4,3,2,1,0:T(8,128)S(1)} %get-tuple-element.287), channel_id=1, source_target_pairs={{16,0},{32,16},{48,32},{64,48},{80,64},{96,80},{112,96},{17,1},{33... | collective-permute-start | bytes 147464 | tf_op jit(solution)/shard_map/ppermute | solution.py:26
  134.1 4.4 collective-permute-start.15
  136.3 5.9 %collective-permute-start.14 = (f32[2,3,16,2,128]{4,3,2,1,0:T(2,128)S(1)}, f32[2,3,16,2,128]{4,3,2,1,0:T(2,128)S(1)}, u32[]{:S(2)}, u32[]{:S(2)}) collective-permute-start(f32[2,3,16,2,128]{4,3,2,1,0:T(2,128)S(1)} %get-tuple-element.289), channel_id=1, source_target_pairs={{1,0},{2,1},{3,2},{4,3},{5,4},{6,5},{7,6},{8,7},{9,8},{10,9},{11,1... | collective-permute-start | bytes 294920 | tf_op jit(solution)/shard_map/ppermute | solution.py:26
  181.9 8.2 %collective-permute-start.17 = (f32[2,3,2,8,128]{4,3,2,1,0:T(8,128)S(1)}, f32[2,3,2,8,128]{4,3,2,1,0:T(8,128)S(1)}, u32[]{:S(2)}, u32[]{:S(2)}) collective-permute-start(f32[2,3,2,8,128]{4,3,2,1,0:T(8,128)S(1)} %get-tuple-element.280), channel_id=1, source_target_pairs={{0,16},{16,32},{32,48},{48,64},{64,80},{80,96},{96,112},{1,17},{17... | collective-permute-start | bytes 147464 | tf_op jit(solution)/shard_map/ppermute | solution.py:25
  183.8 6.2 %collective-permute-start.16 = (f32[2,3,2,8,128]{4,3,2,1,0:T(8,128)S(1)}, f32[2,3,2,8,128]{4,3,2,1,0:T(8,128)S(1)}, u32[]{:S(2)}, u32[]{:S(2)}) collective-permute-start(f32[2,3,2,8,128]{4,3,2,1,0:T(8,128)S(1)} %get-tuple-element.281), channel_id=1, source_target_pairs={{16,0},{32,16},{48,32},{64,48},{80,64},{96,80},{112,96},{17,1},{33... | collective-permute-start | bytes 147464 | tf_op jit(solution)/shard_map/ppermute | solution.py:26
  185.2 5.0 %collective-permute-start.19 = (f32[2,3,16,2,128]{4,3,2,1,0:T(2,128)S(1)}, f32[2,3,16,2,128]{4,3,2,1,0:T(2,128)S(1)}, u32[]{:S(2)}, u32[]{:S(2)}) collective-permute-start(f32[2,3,16,2,128]{4,3,2,1,0:T(2,128)S(1)} %get-tuple-element.282), channel_id=1, source_target_pairs={{0,1},{1,2},{2,3},{3,4},{4,5},{5,6},{6,7},{7,8},{8,9},{9,10},{10,1... | collective-permute-start | bytes 294920 | tf_op jit(solution)/shard_map/ppermute | solution.py:25
  188.1 5.9 %collective-permute-start.18 = (f32[2,3,16,2,128]{4,3,2,1,0:T(2,128)S(1)}, f32[2,3,16,2,128]{4,3,2,1,0:T(2,128)S(1)}, u32[]{:S(2)}, u32[]{:S(2)}) collective-permute-start(f32[2,3,16,2,128]{4,3,2,1,0:T(2,128)S(1)} %get-tuple-element.283), channel_id=1, source_target_pairs={{1,0},{2,1},{3,2},{4,3},{5,4},{6,5},{7,6},{8,7},{9,8},{10,9},{11,1... | collective-permute-start | bytes 294920 | tf_op jit(solution)/shard_map/ppermute | solution.py:26
  237.8 7.8 %collective-permute-start.21 = (f32[2,3,2,8,128]{4,3,2,1,0:T(8,128)S(1)}, f32[2,3,2,8,128]{4,3,2,1,0:T(8,128)S(1)}, u32[]{:S(2)}, u32[]{:S(2)}) collective-permute-start(f32[2,3,2,8,128]{4,3,2,1,0:T(8,128)S(1)} %get-tuple-element.272), channel_id=1, source_target_pairs={{0,16},{16,32},{32,48},{48,64},{64,80},{80,96},{96,112},{1,17},{17... | collective-permute-start | bytes 147464 | tf_op jit(solution)/shard_map/ppermute | solution.py:25
  239.8 5.7 %collective-permute-start.20 = (f32[2,3,2,8,128]{4,3,2,1,0:T(8,128)S(1)}, f32[2,3,2,8,128]{4,3,2,1,0:T(8,128)S(1)}, u32[]{:S(2)}, u32[]{:S(2)}) collective-permute-start(f32[2,3,2,8,128]{4,3,2,1,0:T(8,128)S(1)} %get-tuple-element.273), channel_id=1, source_target_pairs={{16,0},{32,16},{48,32},{64,48},{80,64},{96,80},{112,96},{17,1},{33... | collective-permute-start | bytes 147464 | tf_op jit(solution)/shard_map/ppermute | solution.py:26
  241.2 4.4 collective-permute-start.23
  243.4 5.9 %collective-permute-start.22 = (f32[2,3,16,2,128]{4,3,2,1,0:T(2,128)S(1)}, f32[2,3,16,2,128]{4,3,2,1,0:T(2,128)S(1)}, u32[]{:S(2)}, u32[]{:S(2)}) collective-permute-start(f32[2,3,16,2,128]{4,3,2,1,0:T(2,128)S(1)} %get-tuple-element.275), channel_id=1, source_target_pairs={{1,0},{2,1},{3,2},{4,3},{5,4},{6,5},{7,6},{8,7},{9,8},{10,9},{11,1... | collective-permute-start | bytes 294920 | tf_op jit(solution)/shard_map/ppermute | solution.py:26
  290.6 12.4 %copy-start.2 = (f32[1,3,16,8,128]{4,3,2,1,0:T(8,128)}, f32[1,3,16,8,128]{4,3,2,1,0:T(8,128)S(1)}, u32[]{:S(2)}) copy-start(f32[1,3,16,8,128]{4,3,2,1,0:T(8,128)S(1)} %multiply_add_fusion.8) | copy-start | bytes 589828
  290.8 8.2 %collective-permute-start.25 = (f32[2,3,2,8,128]{4,3,2,1,0:T(8,128)S(1)}, f32[2,3,2,8,128]{4,3,2,1,0:T(8,128)S(1)}, u32[]{:S(2)}, u32[]{:S(2)}) collective-permute-start(f32[2,3,2,8,128]{4,3,2,1,0:T(8,128)S(1)} %get-tuple-element.266), channel_id=1, source_target_pairs={{0,16},{16,32},{32,48},{48,64},{64,80},{80,96},{96,112},{1,17},{17... | collective-permute-start | bytes 147464 | tf_op jit(solution)/shard_map/ppermute | solution.py:25
  292.7 6.2 %collective-permute-start.24 = (f32[2,3,2,8,128]{4,3,2,1,0:T(8,128)S(1)}, f32[2,3,2,8,128]{4,3,2,1,0:T(8,128)S(1)}, u32[]{:S(2)}, u32[]{:S(2)}) collective-permute-start(f32[2,3,2,8,128]{4,3,2,1,0:T(8,128)S(1)} %get-tuple-element.267), channel_id=1, source_target_pairs={{16,0},{32,16},{48,32},{64,48},{80,64},{96,80},{112,96},{17,1},{33... | collective-permute-start | bytes 147464 | tf_op jit(solution)/shard_map/ppermute | solution.py:26
  294.1 4.9 %collective-permute-start.27 = (f32[2,3,16,2,128]{4,3,2,1,0:T(2,128)S(1)}, f32[2,3,16,2,128]{4,3,2,1,0:T(2,128)S(1)}, u32[]{:S(2)}, u32[]{:S(2)}) collective-permute-start(f32[2,3,16,2,128]{4,3,2,1,0:T(2,128)S(1)} %get-tuple-element.268), channel_id=1, source_target_pairs={{0,1},{1,2},{2,3},{3,4},{4,5},{5,6},{6,7},{7,8},{8,9},{9,10},{10,1... | collective-permute-start | bytes 294920 | tf_op jit(solution)/shard_map/ppermute | solution.py:25
  297.0 5.9 %collective-permute-start.26 = (f32[2,3,16,2,128]{4,3,2,1,0:T(2,128)S(1)}, f32[2,3,16,2,128]{4,3,2,1,0:T(2,128)S(1)}, u32[]{:S(2)}, u32[]{:S(2)}) collective-permute-start(f32[2,3,16,2,128]{4,3,2,1,0:T(2,128)S(1)} %get-tuple-element.269), channel_id=1, source_target_pairs={{1,0},{2,1},{3,2},{4,3},{5,4},{6,5},{7,6},{8,7},{9,8},{10,9},{11,1... | collective-permute-start | bytes 294920 | tf_op jit(solution)/shard_map/ppermute | solution.py:26
  304.9 1.7 copy-start.13
  344.5 3.5 copy-start.23
  344.5 3.5 copy-start.25
  349.4 8.0 %collective-permute-start.29 = (f32[2,3,2,8,128]{4,3,2,1,0:T(8,128)S(1)}, f32[2,3,2,8,128]{4,3,2,1,0:T(8,128)S(1)}, u32[]{:S(2)}, u32[]{:S(2)}) collective-permute-start(f32[2,3,2,8,128]{4,3,2,1,0:T(8,128)S(1)} %get-tuple-element.258), channel_id=1, source_target_pairs={{0,16},{16,32},{32,48},{48,64},{64,80},{80,96},{96,112},{1,17},{17... | collective-permute-start | bytes 147464 | tf_op jit(solution)/shard_map/ppermute | solution.py:25
  351.4 5.9 %collective-permute-start.28 = (f32[2,3,2,8,128]{4,3,2,1,0:T(8,128)S(1)}, f32[2,3,2,8,128]{4,3,2,1,0:T(8,128)S(1)}, u32[]{:S(2)}, u32[]{:S(2)}) collective-permute-start(f32[2,3,2,8,128]{4,3,2,1,0:T(8,128)S(1)} %get-tuple-element.259), channel_id=1, source_target_pairs={{16,0},{32,16},{48,32},{64,48},{80,64},{96,80},{112,96},{17,1},{33... | collective-permute-start | bytes 147464 | tf_op jit(solution)/shard_map/ppermute | solution.py:26
  352.8 4.7 %collective-permute-start.31 = (f32[2,3,16,2,128]{4,3,2,1,0:T(2,128)S(1)}, f32[2,3,16,2,128]{4,3,2,1,0:T(2,128)S(1)}, u32[]{:S(2)}, u32[]{:S(2)}) collective-permute-start(f32[2,3,16,2,128]{4,3,2,1,0:T(2,128)S(1)} %get-tuple-element.260), channel_id=1, source_target_pairs={{0,1},{1,2},{2,3},{3,4},{4,5},{5,6},{6,7},{7,8},{8,9},{9,10},{10,1... | collective-permute-start | bytes 294920 | tf_op jit(solution)/shard_map/ppermute | solution.py:25
  355.0 5.9 %collective-permute-start.30 = (f32[2,3,16,2,128]{4,3,2,1,0:T(2,128)S(1)}, f32[2,3,16,2,128]{4,3,2,1,0:T(2,128)S(1)}, u32[]{:S(2)}, u32[]{:S(2)}) collective-permute-start(f32[2,3,16,2,128]{4,3,2,1,0:T(2,128)S(1)} %get-tuple-element.261), channel_id=1, source_target_pairs={{1,0},{2,1},{3,2},{4,3},{5,4},{6,5},{7,6},{8,7},{9,8},{10,9},{11,1... | collective-permute-start | bytes 294920 | tf_op jit(solution)/shard_map/ppermute | solution.py:26
  362.8 36.5 %copy-start.44 = (f32[3]{0:T(128)S(1)}, f32[3]{0:T(128)}, u32[]{:S(2)}) copy-start(f32[3]{0:T(128)} %get-tuple-element.151) | copy-start | bytes 40
  362.8 36.5 %copy-start.45 = (f32[3]{0:T(128)S(1)}, f32[3]{0:T(128)}, u32[]{:S(2)}) copy-start(f32[3]{0:T(128)} %get-tuple-element.152) | copy-start | bytes 40
  403.3 8.2 %collective-permute-start.33 = (f32[2,3,2,8,128]{4,3,2,1,0:T(8,128)S(1)}, f32[2,3,2,8,128]{4,3,2,1,0:T(8,128)S(1)}, u32[]{:S(2)}, u32[]{:S(2)}) collective-permute-start(f32[2,3,2,8,128]{4,3,2,1,0:T(8,128)S(1)} %get-tuple-element.252), channel_id=1, source_target_pairs={{0,16},{16,32},{32,48},{48,64},{64,80},{80,96},{96,112},{1,17},{17... | collective-permute-start | bytes 147464 | tf_op jit(solution)/shard_map/ppermute | solution.py:25
  405.3 6.2 %collective-permute-start.32 = (f32[2,3,2,8,128]{4,3,2,1,0:T(8,128)S(1)}, f32[2,3,2,8,128]{4,3,2,1,0:T(8,128)S(1)}, u32[]{:S(2)}, u32[]{:S(2)}) collective-permute-start(f32[2,3,2,8,128]{4,3,2,1,0:T(8,128)S(1)} %get-tuple-element.253), channel_id=1, source_target_pairs={{16,0},{32,16},{48,32},{64,48},{80,64},{96,80},{112,96},{17,1},{33... | collective-permute-start | bytes 147464 | tf_op jit(solution)/shard_map/ppermute | solution.py:26
  406.7 4.9 %collective-permute-start.35 = (f32[2,3,16,2,128]{4,3,2,1,0:T(2,128)S(1)}, f32[2,3,16,2,128]{4,3,2,1,0:T(2,128)S(1)}, u32[]{:S(2)}, u32[]{:S(2)}) collective-permute-start(f32[2,3,16,2,128]{4,3,2,1,0:T(2,128)S(1)} %get-tuple-element.254), channel_id=1, source_target_pairs={{0,1},{1,2},{2,3},{3,4},{4,5},{5,6},{6,7},{7,8},{8,9},{9,10},{10,1... | collective-permute-start | bytes 294920 | tf_op jit(solution)/shard_map/ppermute | solution.py:25
  409.6 5.9 %collective-permute-start.34 = (f32[2,3,16,2,128]{4,3,2,1,0:T(2,128)S(1)}, f32[2,3,16,2,128]{4,3,2,1,0:T(2,128)S(1)}, u32[]{:S(2)}, u32[]{:S(2)}) collective-permute-start(f32[2,3,16,2,128]{4,3,2,1,0:T(2,128)S(1)} %get-tuple-element.255), channel_id=1, source_target_pairs={{1,0},{2,1},{3,2},{4,3},{5,4},{6,5},{7,6},{8,7},{9,8},{10,9},{11,1... | collective-permute-start | bytes 294920 | tf_op jit(solution)/shard_map/ppermute | solution.py:26
  417.3 39.5 %copy-start.4 = (f32[1,3,16,8,128]{4,3,2,1,0:T(8,128)S(1)}, f32[1,3,16,8,128]{4,3,2,1,0:T(8,128)}, u32[]{:S(2)}) copy-start(f32[1,3,16,8,128]{4,3,2,1,0:T(8,128)} %copy-done.2) | copy-start | bytes 589828
  417.3 39.5 %copy-start.8 = (f32[1,3,16,8,128]{4,3,2,1,0:T(8,128)S(1)}, f32[1,3,16,8,128]{4,3,2,1,0:T(8,128)}, u32[]{:S(2)}) copy-start(f32[1,3,16,8,128]{4,3,2,1,0:T(8,128)} %copy-done.7) | copy-start | bytes 589828
  417.6 39.3 %copy-start.10 = (f32[1,3,16,8,128]{4,3,2,1,0:T(8,128)S(1)}, f32[1,3,16,8,128]{4,3,2,1,0:T(8,128)}, u32[]{:S(2)}) copy-start(f32[1,3,16,8,128]{4,3,2,1,0:T(8,128)} %copy-done.9) | copy-start | bytes 589828
  456.8 2.3 copy-start.28
  456.8 2.3 copy-start.29
  456.8 2.3 copy-start.30
  456.9 2.3 copy-start.31
  456.9 2.3 copy-start.32
  456.9 2.3 copy-start.33
  456.9 2.3 copy-start.34
  456.9 2.3 copy-start.35
  456.9 2.3 copy-start.36
  456.9 2.3 copy-start.37
  456.9 2.3 copy-start.38
  456.9 2.3 copy-start.39
  456.9 2.3 copy-start.40
  457.0 2.3 copy-start.41
  (18 other events, 14.4 us)
where the time goes:
time: 462 us; the launch traced here: 460 us
  blocking collectives  295 us (64%)
  starting transfers between devices  79.9 us (17%)
  other arithmetic  44.2 us (10%)
  waiting for transfers between devices  29.9 us (6%)
  local copies, waits for them, and re-layouts  9.09 us (2%)
    psum x24, blocking collectives, by_axis(): array = lax.psum(array, axis)  295 us
    ppermute x18, starting transfers between devices, padded_2(): lax.ppermute(last, axis, up)  46.7 us
    ppermute x18, starting transfers between devices, padded_2(): lax.ppermute(leading, axis, [(b, a) for a, b in up])  33.3 us
    ppermute x18, waiting for transfers between devices, padded_2(): lax.ppermute(leading, axis, [(b, a) for a, b in up])  29.8 us
    sub x11, other arithmetic, scale_complex(): real_coef * vector[0] - imag_coef * vector[1]  12.4 us
    concatenate x17, other arithmetic, padded_2(): jnp.concatenate([jnp.pad(low, around), array, jnp.pad(high, around)], axi...  10.3 us
  transfers between devices with their start and end apart: 36, of which 8 were waited for; matrix products, arithmetic and copies ran while one was open for 1% of the time, Pallas kernels for 0%

commit v1 on v0

--- a/solution.py
+++ b/solution.py
@@ -36,7 +36,8 @@
 
 def by_axis(array, axes):
     for axis in axes:
-        array = lax.psum(array, axis)
+        parts = lax.all_gather(array, axis, axis=0, tiled=False)
+        array = parts.sum(axis=0)
     return array
 
 

time: 462 us -> 572 us (1.24); the launches traced: 460 us -> 563 us
  local copies, waits for them, and re-layouts: 9.09 us -> 86.7 us
  starting transfers between devices: 79.9 us -> 101 us
  other arithmetic: 44.2 us -> 63.1 us
  waiting for transfers between devices: 29.9 us -> 11.2 us
    unnamed x0 -> x24, blocking collectives: none -> 296 us
    psum x24 -> x0, blocking collectives: 295 us -> none  [by_axis(): array = lax.psum(array, axis)]
    unnamed x94 -> x299, local copies, waits for them, and re-layouts: 6.3 us -> 62.9 us
    ppermute x18, waiting for transfers between devices: 29.8 us -> 1.56 us  [padded_2(): lax.ppermute(leading, axis, [(b, a) for a, b in up])]
    all_gather x0 -> x102, local copies, waits for them, and re-layouts: none -> 21.1 us  [by_axis(): parts = lax.all_gather(array, axis, axis=0, tiled=False)]
    reduce_sum x0 -> x102, other arithmetic: none -> 15.9 us  [by_axis(): array = parts.sum(axis=0)]
    ppermute x18, starting transfers between devices: 46.7 us -> 58.7 us  [padded_2(): lax.ppermute(last, axis, up)]
    ppermute x18, waiting for transfers between devices: 0.05 us -> 9.61 us  [padded_2(): lax.ppermute(last, axis, up)]
  transfers between devices with their start and end apart: 36 -> 36, of which waited for: 8 -> 15; matrix products, arithmetic and copies ran while one was open for 1% -> 1% of each run, Pallas kernels for 0% -> 0%
where the time goes in v1:
time: 572 us; the launch traced here: 563 us
  blocking collectives  296 us (52%)
  starting transfers between devices  101 us (18%)
  local copies, waits for them, and re-layouts  86.7 us (15%)
  other arithmetic  63.1 us (11%)
  waiting for transfers between devices  11.2 us (2%)
    unnamed x24, blocking collectives  296 us
    unnamed x299, local copies, waits for them, and re-layouts  62.9 us
    ppermute x18, starting transfers between devices, padded_2(): lax.ppermute(last, axis, up)  58.7 us
    ppermute x18, starting transfers between devices, padded_2(): lax.ppermute(leading, axis, [(b, a) for a, b in up])  42.7 us
    all_gather x102, local copies, waits for them, and re-layouts, by_axis(): parts = lax.all_gather(array, axis, axis=0, tiled=False)  21.1 us
    reduce_sum x102, other arithmetic, by_axis(): array = parts.sum(axis=0)  15.9 us
    sub x11, other arithmetic, scale_complex(): real_coef * vector[0] - imag_coef * vector[1]  12.4 us
  transfers between devices with their start and end apart: 36, of which 15 were waited for; matrix products, arithmetic and copies ran while one was open for 1% of the time, Pallas kernels for 0%

profile of v1, /device:TPU:1, one launch (start us, length us, event | category | flops | bytes accessed | tf_op | source)
XLA Modules:
  0.0 562.6 jit_solution(7409381312549884526)
XLA Ops:
  1.8 8.7 %collective-permute-start.2 = (f32[2,3,16,2,128]{4,3,2,1,0:T(2,128)S(1)}, f32[2,3,16,2,128]{4,3,2,1,0:T(2,128)S(1)}, u32[]{:S(2)}, u32[]{:S(2)}) collective-permute-start(f32[2,3,16,2,128]{4,3,2,1,0:T(2,128)S(1)} %get-tuple-element.310), channel_id=1, source_target_pairs={{1,0},{2,1},{3,2},{4,3},{5,4},{6,5},{7,6},{8,7},{9,8},{10,9},{11,1... | collective-permute-start | bytes 294920 | tf_op jit(solution)/shard_map/ppermute | solution.py:26
  14.0 1.9 collective-permute-start.3
  27.0 4.6 collective-permute-start.5
  31.7 2.7 collective-permute-start.6
  34.4 2.9 collective-permute-start.7
  41.8 14.0 %all-reduce.144 = (f32[24]{0:T(128)S(1)}, f32[24]{0:T(128)S(1)}, f32[24]{0:T(128)S(1)}, f32[24]{0:T(128)S(1)}) all-reduce(f32[24]{0:T(128)S(1)} %dynamic-update-slice, f32[24]{0:T(128)S(1)} %dynamic-update-slice.9, f32[24]{0:T(128)S(1)} %dynamic-update-slice.6, ...), channel_id=2, replica_groups=mesh['orb'=4,'gx'=8,'gyz_0'=8,'gyz_1'=2] {'gx'}, use_global_device_ids=true, to_apply=%add.27 | all-reduce | flops 96 | bytes 768
  57.2 16.6 %all-reduce.136 = (f32[24]{0:T(128)S(1)}, f32[24]{0:T(128)S(1)}, f32[24]{0:T(128)S(1)}, f32[24]{0:T(128)S(1)}) all-reduce(f32[24]{0:T(128)S(1)} %dynamic-update-slice.1, f32[24]{0:T(128)S(1)} %dynamic-update-slice.10, f32[24]{0:T(128)S(1)} %dynamic-update-slice.7, ...), channel_id=3, replica_groups=mesh['orb'=4,'gx'=8,'gyz_0'=8,'gyz_1'=2] {'gyz_0'}, use_global_device_ids=true, to_apply=%add.28 | all-reduce | flops 96 | bytes 768
  75.1 12.3 %all-reduce.152 = (f32[6]{0:T(128)S(1)}, f32[6]{0:T(128)S(1)}, f32[6]{0:T(128)S(1)}, f32[6]{0:T(128)S(1)}) all-reduce(f32[6]{0:T(128)S(1)} %dynamic-update-slice.2, f32[6]{0:T(128)S(1)} %dynamic-update-slice.11, f32[6]{0:T(128)S(1)} %dynamic-update-slice.8, ...), channel_id=4, replica_groups=mesh['orb'=4,'gx'=8,'gyz_0'=8,'gyz_1'=2] {'gyz_1'}, use_global_device_ids=true, to_apply=%add.29 | all-reduce | flops 24 | bytes 192
  90.2 4.0 collective-permute-start.9
  94.3 2.8 collective-permute-start.10
  97.1 2.9 collective-permute-start.11
  105.4 12.4 %all-reduce.143 = (f32[24]{0:T(128)S(1)}, f32[24]{0:T(128)S(1)}, f32[24]{0:T(128)S(1)}, f32[24]{0:T(128)S(1)}, f32[24]{0:T(128)S(1)}, /*index=5*/f32[24]{0:T(128)S(1)}, f32[24]{0:T(128)S(1)}) all-reduce(f32[24]{0:T(128)S(1)} %dynamic-update-slice.18, ...), channel_id=20, replica_groups=mesh['orb'=4,'gx'=8,'gyz_0'=8,'gyz_1'=2] {'gx'}, use_global_device_ids=true, to_apply=%add.45 | all-reduce | flops 168 | bytes 1344
  120.2 11.2 %all-reduce.135 = (f32[24]{0:T(128)S(1)}, f32[24]{0:T(128)S(1)}, f32[24]{0:T(128)S(1)}, f32[24]{0:T(128)S(1)}, f32[24]{0:T(128)S(1)}, /*index=5*/f32[24]{0:T(128)S(1)}, f32[24]{0:T(128)S(1)}) all-reduce(f32[24]{0:T(128)S(1)} %dynamic-update-slice.19, ...), channel_id=21, replica_groups=mesh['orb'=4,'gx'=8,'gyz_0'=8,'gyz_1'=2] {'gyz_0'}, use_global_device_ids=true, to_apply=%add.46 | all-reduce | flops 168 | bytes 1344
  133.8 11.3 %all-reduce.151 = (f32[6]{0:T(128)S(1)}, f32[6]{0:T(128)S(1)}, f32[6]{0:T(128)S(1)}, f32[6]{0:T(128)S(1)}, f32[6]{0:T(128)S(1)}, /*index=5*/f32[6]{0:T(128)S(1)}, f32[6]{0:T(128)S(1)}) all-reduce(f32[6]{0:T(128)S(1)} %dynamic-update-slice.20, ...), channel_id=22, replica_groups=mesh['orb'=4,'gx'=8,'gyz_0'=8,'gyz_1'=2] {'gyz_1'}, use_global_device_ids=true, to_apply=%add.47 | all-reduce | flops 42 | bytes 336
  149.2 4.0 collective-permute-start.13
  153.3 2.8 collective-permute-start.14
  156.1 2.8 collective-permute-start.15
  162.9 12.4 %all-reduce.142 = (f32[24]{0:T(128)S(1)}, f32[24]{0:T(128)S(1)}) all-reduce(f32[24]{0:T(128)S(1)} %dynamic-update-slice.36, f32[24]{0:T(128)S(1)} %dynamic-update-slice.33), channel_id=38, replica_groups=mesh['orb'=4,'gx'=8,'gyz_0'=8,'gyz_1'=2] {'gx'}, use_global_device_ids=true, to_apply=%add.63 | all-reduce | flops 48 | bytes 384
  176.0 12.5 %all-reduce.134 = (f32[24]{0:T(128)S(1)}, f32[24]{0:T(128)S(1)}) all-reduce(f32[24]{0:T(128)S(1)} %dynamic-update-slice.37, f32[24]{0:T(128)S(1)} %dynamic-update-slice.34), channel_id=39, replica_groups=mesh['orb'=4,'gx'=8,'gyz_0'=8,'gyz_1'=2] {'gyz_0'}, use_global_device_ids=true, to_apply=%add.64 | all-reduce | flops 48 | bytes 384
  189.2 10.8 %all-reduce.150 = (f32[6]{0:T(128)S(1)}, f32[6]{0:T(128)S(1)}) all-reduce(f32[6]{0:T(128)S(1)} %dynamic-update-slice.38, f32[6]{0:T(128)S(1)} %dynamic-update-slice.35), channel_id=40, replica_groups=mesh['orb'=4,'gx'=8,'gyz_0'=8,'gyz_1'=2] {'gyz_1'}, use_global_device_ids=true, to_apply=%add.65 | all-reduce | flops 12 | bytes 96
  203.2 4.0 collective-permute-start.17
  207.2 2.8 collective-permute-start.18
  210.1 2.8 collective-permute-start.19
  221.4 12.4 %all-reduce.141 = (f32[24]{0:T(128)S(1)}, f32[24]{0:T(128)S(1)}, f32[24]{0:T(128)S(1)}, f32[24]{0:T(128)S(1)}, f32[24]{0:T(128)S(1)}, /*index=5*/f32[24]{0:T(128)S(1)}, f32[24]{0:T(128)S(1)}) all-reduce(f32[24]{0:T(128)S(1)} %dynamic-update-slice.45, ...), channel_id=47, replica_groups=mesh['orb'=4,'gx'=8,'gyz_0'=8,'gyz_1'=2] {'gx'}, use_global_device_ids=true, to_apply=%add.72 | all-reduce | flops 168 | bytes 1344
  236.2 12.8 %all-reduce.133 = (f32[24]{0:T(128)S(1)}, f32[24]{0:T(128)S(1)}, f32[24]{0:T(128)S(1)}, f32[24]{0:T(128)S(1)}, f32[24]{0:T(128)S(1)}, /*index=5*/f32[24]{0:T(128)S(1)}, f32[24]{0:T(128)S(1)}) all-reduce(f32[24]{0:T(128)S(1)} %dynamic-update-slice.46, ...), channel_id=48, replica_groups=mesh['orb'=4,'gx'=8,'gyz_0'=8,'gyz_1'=2] {'gyz_0'}, use_global_device_ids=true, to_apply=%add.73 | all-reduce | flops 168 | bytes 1344
  251.5 10.9 %all-reduce.149 = (f32[6]{0:T(128)S(1)}, f32[6]{0:T(128)S(1)}, f32[6]{0:T(128)S(1)}, f32[6]{0:T(128)S(1)}, f32[6]{0:T(128)S(1)}, /*index=5*/f32[6]{0:T(128)S(1)}, f32[6]{0:T(128)S(1)}) all-reduce(f32[6]{0:T(128)S(1)} %dynamic-update-slice.47, ...), channel_id=49, replica_groups=mesh['orb'=4,'gx'=8,'gyz_0'=8,'gyz_1'=2] {'gyz_1'}, use_global_device_ids=true, to_apply=%add.74 | all-reduce | flops 42 | bytes 336
  263.8 2.1 multiply_subtract_fusion.12
  269.2 4.0 collective-permute-start.21
  273.2 2.8 collective-permute-start.22
  276.1 3.2 collective-permute-start.23
  283.7 12.2 %all-reduce.140 = (f32[24]{0:T(128)S(1)}, f32[24]{0:T(128)S(1)}) all-reduce(f32[24]{0:T(128)S(1)} %dynamic-update-slice.63, f32[24]{0:T(128)S(1)} %dynamic-update-slice.60), channel_id=65, replica_groups=mesh['orb'=4,'gx'=8,'gyz_0'=8,'gyz_1'=2] {'gx'}, use_global_device_ids=true, to_apply=%add.90 | all-reduce | flops 48 | bytes 384
  296.5 12.9 %all-reduce.132 = (f32[24]{0:T(128)S(1)}, f32[24]{0:T(128)S(1)}) all-reduce(f32[24]{0:T(128)S(1)} %dynamic-update-slice.64, f32[24]{0:T(128)S(1)} %dynamic-update-slice.61), channel_id=66, replica_groups=mesh['orb'=4,'gx'=8,'gyz_0'=8,'gyz_1'=2] {'gyz_0'}, use_global_device_ids=true, to_apply=%add.91 | all-reduce | flops 48 | bytes 384
  310.1 10.8 %all-reduce.148 = (f32[6]{0:T(128)S(1)}, f32[6]{0:T(128)S(1)}) all-reduce(f32[6]{0:T(128)S(1)} %dynamic-update-slice.65, f32[6]{0:T(128)S(1)} %dynamic-update-slice.62), channel_id=67, replica_groups=mesh['orb'=4,'gx'=8,'gyz_0'=8,'gyz_1'=2] {'gyz_1'}, use_global_device_ids=true, to_apply=%add.92 | all-reduce | flops 12 | bytes 96
  321.2 1.9 multiply_subtract_fusion.8
  325.3 4.0 collective-permute-start.25
  329.4 2.8 collective-permute-start.26
  332.2 2.8 collective-permute-start.27
  341.8 1.7 fusion.82
  344.1 1.4 dynamic-update-slice.69
  346.0 1.4 dynamic-update-slice.66
  351.1 13.1 %all-reduce.139 = (f32[24]{0:T(128)}, f32[24]{0:T(128)}, f32[24]{0:T(128)S(1)}, f32[24]{0:T(128)S(1)}, f32[24]{0:T(128)S(1)}, /*index=5*/f32[24]{0:T(128)S(1)}, f32[24]{0:T(128)}) all-reduce(f32[24]{0:T(128)} %dynamic-update-slice.72, f32[24]{0:T(128)} %dynamic-update-slice.69, ...), channel_id=74, replica_groups=mesh['orb'=4,'gx'=8,'gyz_0'=8,'gyz_1'=2] {'gx'}, use_global_device_ids=true, to_apply=%add.99 | all-reduce | flops 168 | bytes 1344
  373.3 1.3 dynamic-update-slice.70
  378.7 1.4 dynamic-update-slice.76
  380.7 1.4 dynamic-update-slice.82
  385.4 13.5 %all-reduce.131 = (f32[24]{0:T(128)}, f32[24]{0:T(128)}, f32[24]{0:T(128)S(1)}, f32[24]{0:T(128)S(1)}, f32[24]{0:T(128)S(1)}, /*index=5*/f32[24]{0:T(128)S(1)}, f32[24]{0:T(128)}) all-reduce(f32[24]{0:T(128)} %dynamic-update-slice.73, f32[24]{0:T(128)} %dynamic-update-slice.70, ...), channel_id=75, replica_groups=mesh['orb'=4,'gx'=8,'gyz_0'=8,'gyz_1'=2] {'gyz_0'}, use_global_device_ids=true, to_apply=%add.100 | all-reduce | flops 168 | bytes 1344
  404.8 1.3 dynamic-update-slice.74
  407.9 1.4 dynamic-update-slice.71
  411.1 1.4 dynamic-update-slice.68
  416.9 11.6 %all-reduce.147 = (f32[6]{0:T(128)S(1)}, f32[6]{0:T(128)}, f32[6]{0:T(128)}, f32[6]{0:T(128)}, f32[6]{0:T(128)}, /*index=5*/f32[6]{0:T(128)}, f32[6]{0:T(128)S(1)}) all-reduce(f32[6]{0:T(128)} %dynamic-update-slice.74, f32[6]{0:T(128)} %dynamic-update-slice.71, ...), channel_id=76, replica_groups=mesh['orb'=4,'gx'=8,'gyz_0'=8,'gyz_1'=2] {'gyz_1'}, use_global_device_ids=true, to_apply=%add.101 | all-reduce | flops 42 | bytes 336
  441.5 2.2 multiply_subtract_fusion.6
  446.3 4.0 collective-permute-start.29
  450.4 2.8 collective-permute-start.30
  453.2 2.9 collective-permute-start.31
  460.5 12.2 %all-reduce.138 = (f32[24]{0:T(128)S(1)}, f32[24]{0:T(128)S(1)}) all-reduce(f32[24]{0:T(128)S(1)} %dynamic-update-slice.90, f32[24]{0:T(128)S(1)} %dynamic-update-slice.87), channel_id=92, replica_groups=mesh['orb'=4,'gx'=8,'gyz_0'=8,'gyz_1'=2] {'gx'}, use_global_device_ids=true, to_apply=%add.117 | all-reduce | flops 48 | bytes 384
  473.3 12.9 %all-reduce.130 = (f32[24]{0:T(128)S(1)}, f32[24]{0:T(128)S(1)}) all-reduce(f32[24]{0:T(128)S(1)} %dynamic-update-slice.91, f32[24]{0:T(128)S(1)} %dynamic-update-slice.88), channel_id=93, replica_groups=mesh['orb'=4,'gx'=8,'gyz_0'=8,'gyz_1'=2] {'gyz_0'}, use_global_device_ids=true, to_apply=%add.118 | all-reduce | flops 48 | bytes 384
  486.9 10.8 %all-reduce.146 = (f32[6]{0:T(128)S(1)}, f32[6]{0:T(128)S(1)}) all-reduce(f32[6]{0:T(128)S(1)} %dynamic-update-slice.92, f32[6]{0:T(128)S(1)} %dynamic-update-slice.89), channel_id=94, replica_groups=mesh['orb'=4,'gx'=8,'gyz_0'=8,'gyz_1'=2] {'gyz_1'}, use_global_device_ids=true, to_apply=%add.119 | all-reduce | flops 12 | bytes 96
  498.0 2.0 multiply_subtract_fusion.2
  503.3 4.0 collective-permute-start.33
  507.4 2.8 collective-permute-start.34
  510.2 2.8 collective-permute-start.35
  519.3 12.4 %all-reduce.137 = (f32[24]{0:T(128)S(1)}, f32[24]{0:T(128)S(1)}, f32[24]{0:T(128)S(1)}) all-reduce(f32[24]{0:T(128)S(1)} %dynamic-update-slice.99, f32[24]{0:T(128)S(1)} %dynamic-update-slice.96, f32[24]{0:T(128)S(1)} %dynamic-update-slice.93), channel_id=101, replica_groups=mesh['orb'=4,'gx'=8,'gyz_0'=8,'gyz_1'=2] {'gx'}, use_global_device_ids=true, to_apply=%add.126 | all-reduce | flops 72 | bytes 576
  532.7 12.8 %all-reduce.129 = (f32[24]{0:T(128)S(1)}, f32[24]{0:T(128)S(1)}, f32[24]{0:T(128)S(1)}) all-reduce(f32[24]{0:T(128)S(1)} %dynamic-update-slice.100, f32[24]{0:T(128)S(1)} %dynamic-update-slice.97, f32[24]{0:T(128)S(1)} %dynamic-update-slice.94), channel_id=102, replica_groups=mesh['orb'=4,'gx'=8,'gyz_0'=8,'gyz_1'=2] {'gyz_0'}, use_global_device_ids=true, to_apply=%add.127 | all-reduce | flops 72 | bytes 576
  546.5 10.9 %all-reduce.145 = (f32[6]{0:T(128)S(1)}, f32[6]{0:T(128)S(1)}, f32[6]{0:T(128)S(1)}) all-reduce(f32[6]{0:T(128)S(1)} %dynamic-update-slice.101, f32[6]{0:T(128)S(1)} %dynamic-update-slice.98, f32[6]{0:T(128)S(1)} %dynamic-update-slice.95), channel_id=103, replica_groups=mesh['orb'=4,'gx'=8,'gyz_0'=8,'gyz_1'=2] {'gyz_1'}, use_global_device_ids=true, to_apply=%add.128 | all-reduce | flops 18 | bytes 144
  559.1 2.2 maximum_subtract_fusion.10
  (666 shorter events, 150.9 us)
Async XLA Ops:
  1.8 21.9 %collective-permute-start.2 = (f32[2,3,16,2,128]{4,3,2,1,0:T(2,128)S(1)}, f32[2,3,16,2,128]{4,3,2,1,0:T(2,128)S(1)}, u32[]{:S(2)}, u32[]{:S(2)}) collective-permute-start(f32[2,3,16,2,128]{4,3,2,1,0:T(2,128)S(1)} %get-tuple-element.310), channel_id=1, source_target_pairs={{1,0},{2,1},{3,2},{4,3},{5,4},{6,5},{7,6},{8,7},{9,8},{10,9},{11,1... | collective-permute-start | bytes 294920 | tf_op jit(solution)/shard_map/ppermute | solution.py:26
  11.4 11.1 %collective-permute-start.1 = (f32[2,3,2,8,128]{4,3,2,1,0:T(8,128)S(1)}, f32[2,3,2,8,128]{4,3,2,1,0:T(8,128)S(1)}, u32[]{:S(2)}, u32[]{:S(2)}) collective-permute-start(f32[2,3,2,8,128]{4,3,2,1,0:T(8,128)S(1)} %get-tuple-element.312), channel_id=1, source_target_pairs={{0,16},{16,32},{32,48},{48,64},{64,80},{80,96},{96,112},{1,17},{17... | collective-permute-start | bytes 147464 | tf_op jit(solution)/shard_map/ppermute | solution.py:25
  12.7 11.0 %collective-permute-start = (f32[2,3,2,8,128]{4,3,2,1,0:T(8,128)S(1)}, f32[2,3,2,8,128]{4,3,2,1,0:T(8,128)S(1)}, u32[]{:S(2)}, u32[]{:S(2)}) collective-permute-start(f32[2,3,2,8,128]{4,3,2,1,0:T(8,128)S(1)} %get-tuple-element.311), channel_id=1, source_target_pairs={{16,0},{32,16},{48,32},{64,48},{80,64},{96,80},{112,96},{17,1},{33... | collective-permute-start | bytes 147464 | tf_op jit(solution)/shard_map/ppermute | solution.py:26
  14.0 9.8 %collective-permute-start.3 = (f32[2,3,16,2,128]{4,3,2,1,0:T(2,128)S(1)}, f32[2,3,16,2,128]{4,3,2,1,0:T(2,128)S(1)}, u32[]{:S(2)}, u32[]{:S(2)}) collective-permute-start(f32[2,3,16,2,128]{4,3,2,1,0:T(2,128)S(1)} %get-tuple-element.309), channel_id=1, source_target_pairs={{0,1},{1,2},{2,3},{3,4},{4,5},{5,6},{6,7},{7,8},{8,9},{9,10},{10,1... | collective-permute-start | bytes 294920 | tf_op jit(solution)/shard_map/ppermute | solution.py:25
  23.7 1.3 copy-start
  25.7 11.6 %collective-permute-start.4 = (f32[2,3,2,8,128]{4,3,2,1,0:T(8,128)S(1)}, f32[2,3,2,8,128]{4,3,2,1,0:T(8,128)S(1)}, u32[]{:S(2)}, u32[]{:S(2)}) collective-permute-start(f32[2,3,2,8,128]{4,3,2,1,0:T(8,128)S(1)} %get-tuple-element.303), channel_id=1, source_target_pairs={{16,0},{32,16},{48,32},{64,48},{80,64},{96,80},{112,96},{17,1},{33... | collective-permute-start | bytes 147464 | tf_op jit(solution)/shard_map/ppermute | solution.py:26
  27.0 10.3 %collective-permute-start.5 = (f32[2,3,2,8,128]{4,3,2,1,0:T(8,128)S(1)}, f32[2,3,2,8,128]{4,3,2,1,0:T(8,128)S(1)}, u32[]{:S(2)}, u32[]{:S(2)}) collective-permute-start(f32[2,3,2,8,128]{4,3,2,1,0:T(8,128)S(1)} %get-tuple-element.302), channel_id=1, source_target_pairs={{0,16},{16,32},{32,48},{48,64},{64,80},{80,96},{96,112},{1,17},{17... | collective-permute-start | bytes 147464 | tf_op jit(solution)/shard_map/ppermute | solution.py:25
  31.7 5.9 %collective-permute-start.6 = (f32[2,3,16,2,128]{4,3,2,1,0:T(2,128)S(1)}, f32[2,3,16,2,128]{4,3,2,1,0:T(2,128)S(1)}, u32[]{:S(2)}, u32[]{:S(2)}) collective-permute-start(f32[2,3,16,2,128]{4,3,2,1,0:T(2,128)S(1)} %get-tuple-element.305), channel_id=1, source_target_pairs={{1,0},{2,1},{3,2},{4,3},{5,4},{6,5},{7,6},{8,7},{9,8},{10,9},{11,1... | collective-permute-start | bytes 294920 | tf_op jit(solution)/shard_map/ppermute | solution.py:26
  34.4 4.5 collective-permute-start.7
  88.9 11.1 %collective-permute-start.8 = (f32[2,3,2,8,128]{4,3,2,1,0:T(8,128)S(1)}, f32[2,3,2,8,128]{4,3,2,1,0:T(8,128)S(1)}, u32[]{:S(2)}, u32[]{:S(2)}) collective-permute-start(f32[2,3,2,8,128]{4,3,2,1,0:T(8,128)S(1)} %get-tuple-element.295), channel_id=1, source_target_pairs={{16,0},{32,16},{48,32},{64,48},{80,64},{96,80},{112,96},{17,1},{33... | collective-permute-start | bytes 147464 | tf_op jit(solution)/shard_map/ppermute | solution.py:26
  90.2 9.8 %collective-permute-start.9 = (f32[2,3,2,8,128]{4,3,2,1,0:T(8,128)S(1)}, f32[2,3,2,8,128]{4,3,2,1,0:T(8,128)S(1)}, u32[]{:S(2)}, u32[]{:S(2)}) collective-permute-start(f32[2,3,2,8,128]{4,3,2,1,0:T(8,128)S(1)} %get-tuple-element.294), channel_id=1, source_target_pairs={{0,16},{16,32},{32,48},{48,64},{64,80},{80,96},{96,112},{1,17},{17... | collective-permute-start | bytes 147464 | tf_op jit(solution)/shard_map/ppermute | solution.py:25
  94.3 5.9 %collective-permute-start.10 = (f32[2,3,16,2,128]{4,3,2,1,0:T(2,128)S(1)}, f32[2,3,16,2,128]{4,3,2,1,0:T(2,128)S(1)}, u32[]{:S(2)}, u32[]{:S(2)}) collective-permute-start(f32[2,3,16,2,128]{4,3,2,1,0:T(2,128)S(1)} %get-tuple-element.297), channel_id=1, source_target_pairs={{1,0},{2,1},{3,2},{4,3},{5,4},{6,5},{7,6},{8,7},{9,8},{10,9},{11,1... | collective-permute-start | bytes 294920 | tf_op jit(solution)/shard_map/ppermute | solution.py:26
  97.1 4.4 collective-permute-start.11
  145.9 54.4 %copy-start.41 = (f32[3]{0:T(128)}, f32[3]{0:T(128)S(1)}, u32[]{:S(2)}) copy-start(f32[3]{0:T(128)S(1)} %get-tuple-element.175) | copy-start | bytes 40
  145.9 54.4 %copy-start.42 = (f32[3]{0:T(128)}, f32[3]{0:T(128)S(1)}, u32[]{:S(2)}) copy-start(f32[3]{0:T(128)S(1)} %get-tuple-element.176) | copy-start | bytes 40
  147.1 6.2 %copy-start.15 = (f32[1,3,16,8,128]{4,3,2,1,0:T(8,128)}, f32[1,3,16,8,128]{4,3,2,1,0:T(8,128)S(1)}, u32[]{:S(2)}) copy-start(f32[1,3,16,8,128]{4,3,2,1,0:T(8,128)S(1)} %get-tuple-element.240) | copy-start | bytes 589828
  147.9 11.0 %collective-permute-start.12 = (f32[2,3,2,8,128]{4,3,2,1,0:T(8,128)S(1)}, f32[2,3,2,8,128]{4,3,2,1,0:T(8,128)S(1)}, u32[]{:S(2)}, u32[]{:S(2)}) collective-permute-start(f32[2,3,2,8,128]{4,3,2,1,0:T(8,128)S(1)} %get-tuple-element.287), channel_id=1, source_target_pairs={{16,0},{32,16},{48,32},{64,48},{80,64},{96,80},{112,96},{17,1},{33... | collective-permute-start | bytes 147464 | tf_op jit(solution)/shard_map/ppermute | solution.py:26
  149.2 9.7 %collective-permute-start.13 = (f32[2,3,2,8,128]{4,3,2,1,0:T(8,128)S(1)}, f32[2,3,2,8,128]{4,3,2,1,0:T(8,128)S(1)}, u32[]{:S(2)}, u32[]{:S(2)}) collective-permute-start(f32[2,3,2,8,128]{4,3,2,1,0:T(8,128)S(1)} %get-tuple-element.286), channel_id=1, source_target_pairs={{0,16},{16,32},{32,48},{48,64},{64,80},{80,96},{96,112},{1,17},{17... | collective-permute-start | bytes 147464 | tf_op jit(solution)/shard_map/ppermute | solution.py:25
  153.3 5.9 %collective-permute-start.14 = (f32[2,3,16,2,128]{4,3,2,1,0:T(2,128)S(1)}, f32[2,3,16,2,128]{4,3,2,1,0:T(2,128)S(1)}, u32[]{:S(2)}, u32[]{:S(2)}) collective-permute-start(f32[2,3,16,2,128]{4,3,2,1,0:T(2,128)S(1)} %get-tuple-element.289), channel_id=1, source_target_pairs={{1,0},{2,1},{3,2},{4,3},{5,4},{6,5},{7,6},{8,7},{9,8},{10,9},{11,1... | collective-permute-start | bytes 294920 | tf_op jit(solution)/shard_map/ppermute | solution.py:26
  156.1 4.4 collective-permute-start.15
  201.9 10.9 %collective-permute-start.16 = (f32[2,3,2,8,128]{4,3,2,1,0:T(8,128)S(1)}, f32[2,3,2,8,128]{4,3,2,1,0:T(8,128)S(1)}, u32[]{:S(2)}, u32[]{:S(2)}) collective-permute-start(f32[2,3,2,8,128]{4,3,2,1,0:T(8,128)S(1)} %get-tuple-element.281), channel_id=1, source_target_pairs={{16,0},{32,16},{48,32},{64,48},{80,64},{96,80},{112,96},{17,1},{33... | collective-permute-start | bytes 147464 | tf_op jit(solution)/shard_map/ppermute | solution.py:26
  203.2 9.7 %collective-permute-start.17 = (f32[2,3,2,8,128]{4,3,2,1,0:T(8,128)S(1)}, f32[2,3,2,8,128]{4,3,2,1,0:T(8,128)S(1)}, u32[]{:S(2)}, u32[]{:S(2)}) collective-permute-start(f32[2,3,2,8,128]{4,3,2,1,0:T(8,128)S(1)} %get-tuple-element.280), channel_id=1, source_target_pairs={{0,16},{16,32},{32,48},{48,64},{64,80},{80,96},{96,112},{1,17},{17... | collective-permute-start | bytes 147464 | tf_op jit(solution)/shard_map/ppermute | solution.py:25
  207.2 5.9 %collective-permute-start.18 = (f32[2,3,16,2,128]{4,3,2,1,0:T(2,128)S(1)}, f32[2,3,16,2,128]{4,3,2,1,0:T(2,128)S(1)}, u32[]{:S(2)}, u32[]{:S(2)}) collective-permute-start(f32[2,3,16,2,128]{4,3,2,1,0:T(2,128)S(1)} %get-tuple-element.283), channel_id=1, source_target_pairs={{1,0},{2,1},{3,2},{4,3},{5,4},{6,5},{7,6},{8,7},{9,8},{10,9},{11,1... | collective-permute-start | bytes 294920 | tf_op jit(solution)/shard_map/ppermute | solution.py:26
  210.1 4.4 collective-permute-start.19
  216.3 47.5 %copy-start.10 = (f32[1,3,16,8,128]{4,3,2,1,0:T(8,128)}, f32[1,3,16,8,128]{4,3,2,1,0:T(8,128)S(1)}, u32[]{:S(2)}) copy-start(f32[1,3,16,8,128]{4,3,2,1,0:T(8,128)S(1)} %get-tuple-element.277) | copy-start | bytes 589828
  263.8 57.3 %copy-start.39 = (f32[3]{0:T(128)}, f32[3]{0:T(128)S(1)}, u32[]{:S(2)}) copy-start(f32[3]{0:T(128)S(1)} %get-tuple-element.163) | copy-start | bytes 40
  263.8 57.3 %copy-start.40 = (f32[3]{0:T(128)}, f32[3]{0:T(128)S(1)}, u32[]{:S(2)}) copy-start(f32[3]{0:T(128)S(1)} %get-tuple-element.164) | copy-start | bytes 40
  267.9 11.3 %collective-permute-start.20 = (f32[2,3,2,8,128]{4,3,2,1,0:T(8,128)S(1)}, f32[2,3,2,8,128]{4,3,2,1,0:T(8,128)S(1)}, u32[]{:S(2)}, u32[]{:S(2)}) collective-permute-start(f32[2,3,2,8,128]{4,3,2,1,0:T(8,128)S(1)} %get-tuple-element.273), channel_id=1, source_target_pairs={{16,0},{32,16},{48,32},{64,48},{80,64},{96,80},{112,96},{17,1},{33... | collective-permute-start | bytes 147464 | tf_op jit(solution)/shard_map/ppermute | solution.py:26
  269.2 10.1 %collective-permute-start.21 = (f32[2,3,2,8,128]{4,3,2,1,0:T(8,128)S(1)}, f32[2,3,2,8,128]{4,3,2,1,0:T(8,128)S(1)}, u32[]{:S(2)}, u32[]{:S(2)}) collective-permute-start(f32[2,3,2,8,128]{4,3,2,1,0:T(8,128)S(1)} %get-tuple-element.272), channel_id=1, source_target_pairs={{0,16},{16,32},{32,48},{48,64},{64,80},{80,96},{96,112},{1,17},{17... | collective-permute-start | bytes 147464 | tf_op jit(solution)/shard_map/ppermute | solution.py:25
  273.2 6.1 %collective-permute-start.22 = (f32[2,3,16,2,128]{4,3,2,1,0:T(2,128)S(1)}, f32[2,3,16,2,128]{4,3,2,1,0:T(2,128)S(1)}, u32[]{:S(2)}, u32[]{:S(2)}) collective-permute-start(f32[2,3,16,2,128]{4,3,2,1,0:T(2,128)S(1)} %get-tuple-element.275), channel_id=1, source_target_pairs={{1,0},{2,1},{3,2},{4,3},{5,4},{6,5},{7,6},{8,7},{9,8},{10,9},{11,1... | collective-permute-start | bytes 294920 | tf_op jit(solution)/shard_map/ppermute | solution.py:26
  276.1 4.4 collective-permute-start.23
  321.1 2.1 copy-start.37
  321.1 2.1 copy-start.38
  323.8 12.8 %copy-start.2 = (f32[1,3,16,8,128]{4,3,2,1,0:T(8,128)}, f32[1,3,16,8,128]{4,3,2,1,0:T(8,128)S(1)}, u32[]{:S(2)}) copy-start(f32[1,3,16,8,128]{4,3,2,1,0:T(8,128)S(1)} %multiply_add_fusion.8) | copy-start | bytes 589828
  324.0 11.0 %collective-permute-start.24 = (f32[2,3,2,8,128]{4,3,2,1,0:T(8,128)S(1)}, f32[2,3,2,8,128]{4,3,2,1,0:T(8,128)S(1)}, u32[]{:S(2)}, u32[]{:S(2)}) collective-permute-start(f32[2,3,2,8,128]{4,3,2,1,0:T(8,128)S(1)} %get-tuple-element.267), channel_id=1, source_target_pairs={{16,0},{32,16},{48,32},{64,48},{80,64},{96,80},{112,96},{17,1},{33... | collective-permute-start | bytes 147464 | tf_op jit(solution)/shard_map/ppermute | solution.py:26
  325.3 9.7 %collective-permute-start.25 = (f32[2,3,2,8,128]{4,3,2,1,0:T(8,128)S(1)}, f32[2,3,2,8,128]{4,3,2,1,0:T(8,128)S(1)}, u32[]{:S(2)}, u32[]{:S(2)}) collective-permute-start(f32[2,3,2,8,128]{4,3,2,1,0:T(8,128)S(1)} %get-tuple-element.266), channel_id=1, source_target_pairs={{0,16},{16,32},{32,48},{48,64},{64,80},{80,96},{96,112},{1,17},{17... | collective-permute-start | bytes 147464 | tf_op jit(solution)/shard_map/ppermute | solution.py:25
  329.4 5.9 %collective-permute-start.26 = (f32[2,3,16,2,128]{4,3,2,1,0:T(2,128)S(1)}, f32[2,3,16,2,128]{4,3,2,1,0:T(2,128)S(1)}, u32[]{:S(2)}, u32[]{:S(2)}) collective-permute-start(f32[2,3,16,2,128]{4,3,2,1,0:T(2,128)S(1)} %get-tuple-element.269), channel_id=1, source_target_pairs={{1,0},{2,1},{3,2},{4,3},{5,4},{6,5},{7,6},{8,7},{9,8},{10,9},{11,1... | collective-permute-start | bytes 294920 | tf_op jit(solution)/shard_map/ppermute | solution.py:26
  332.2 4.4 collective-permute-start.27
  440.7 3.0 copy-start.18
  440.7 3.0 copy-start.20
  445.0 11.1 %collective-permute-start.28 = (f32[2,3,2,8,128]{4,3,2,1,0:T(8,128)S(1)}, f32[2,3,2,8,128]{4,3,2,1,0:T(8,128)S(1)}, u32[]{:S(2)}, u32[]{:S(2)}) collective-permute-start(f32[2,3,2,8,128]{4,3,2,1,0:T(8,128)S(1)} %get-tuple-element.259), channel_id=1, source_target_pairs={{16,0},{32,16},{48,32},{64,48},{80,64},{96,80},{112,96},{17,1},{33... | collective-permute-start | bytes 147464 | tf_op jit(solution)/shard_map/ppermute | solution.py:26
  446.3 9.8 %collective-permute-start.29 = (f32[2,3,2,8,128]{4,3,2,1,0:T(8,128)S(1)}, f32[2,3,2,8,128]{4,3,2,1,0:T(8,128)S(1)}, u32[]{:S(2)}, u32[]{:S(2)}) collective-permute-start(f32[2,3,2,8,128]{4,3,2,1,0:T(8,128)S(1)} %get-tuple-element.258), channel_id=1, source_target_pairs={{0,16},{16,32},{32,48},{48,64},{64,80},{80,96},{96,112},{1,17},{17... | collective-permute-start | bytes 147464 | tf_op jit(solution)/shard_map/ppermute | solution.py:25
  450.4 5.9 %collective-permute-start.30 = (f32[2,3,16,2,128]{4,3,2,1,0:T(2,128)S(1)}, f32[2,3,16,2,128]{4,3,2,1,0:T(2,128)S(1)}, u32[]{:S(2)}, u32[]{:S(2)}) collective-permute-start(f32[2,3,16,2,128]{4,3,2,1,0:T(2,128)S(1)} %get-tuple-element.261), channel_id=1, source_target_pairs={{1,0},{2,1},{3,2},{4,3},{5,4},{6,5},{7,6},{8,7},{9,8},{10,9},{11,1... | collective-permute-start | bytes 294920 | tf_op jit(solution)/shard_map/ppermute | solution.py:26
  453.2 4.4 collective-permute-start.31
  502.0 11.0 %collective-permute-start.32 = (f32[2,3,2,8,128]{4,3,2,1,0:T(8,128)S(1)}, f32[2,3,2,8,128]{4,3,2,1,0:T(8,128)S(1)}, u32[]{:S(2)}, u32[]{:S(2)}) collective-permute-start(f32[2,3,2,8,128]{4,3,2,1,0:T(8,128)S(1)} %get-tuple-element.253), channel_id=1, source_target_pairs={{16,0},{32,16},{48,32},{64,48},{80,64},{96,80},{112,96},{17,1},{33... | collective-permute-start | bytes 147464 | tf_op jit(solution)/shard_map/ppermute | solution.py:26
  503.3 9.7 %collective-permute-start.33 = (f32[2,3,2,8,128]{4,3,2,1,0:T(8,128)S(1)}, f32[2,3,2,8,128]{4,3,2,1,0:T(8,128)S(1)}, u32[]{:S(2)}, u32[]{:S(2)}) collective-permute-start(f32[2,3,2,8,128]{4,3,2,1,0:T(8,128)S(1)} %get-tuple-element.252), channel_id=1, source_target_pairs={{0,16},{16,32},{32,48},{48,64},{64,80},{80,96},{96,112},{1,17},{17... | collective-permute-start | bytes 147464 | tf_op jit(solution)/shard_map/ppermute | solution.py:25
  507.4 5.9 %collective-permute-start.34 = (f32[2,3,16,2,128]{4,3,2,1,0:T(2,128)S(1)}, f32[2,3,16,2,128]{4,3,2,1,0:T(2,128)S(1)}, u32[]{:S(2)}, u32[]{:S(2)}) collective-permute-start(f32[2,3,16,2,128]{4,3,2,1,0:T(2,128)S(1)} %get-tuple-element.255), channel_id=1, source_target_pairs={{1,0},{2,1},{3,2},{4,3},{5,4},{6,5},{7,6},{8,7},{9,8},{10,9},{11,1... | collective-permute-start | bytes 294920 | tf_op jit(solution)/shard_map/ppermute | solution.py:26
  510.2 4.4 collective-permute-start.35
  516.4 42.6 %copy-start.4 = (f32[1,3,16,8,128]{4,3,2,1,0:T(8,128)S(1)}, f32[1,3,16,8,128]{4,3,2,1,0:T(8,128)}, u32[]{:S(2)}) copy-start(f32[1,3,16,8,128]{4,3,2,1,0:T(8,128)} %copy-done.2) | copy-start | bytes 589828
  516.4 42.6 %copy-start.8 = (f32[1,3,16,8,128]{4,3,2,1,0:T(8,128)S(1)}, f32[1,3,16,8,128]{4,3,2,1,0:T(8,128)}, u32[]{:S(2)}) copy-start(f32[1,3,16,8,128]{4,3,2,1,0:T(8,128)} %copy-done.7) | copy-start | bytes 589828
  559.0 2.4 copy-start.23
  559.0 2.4 copy-start.24
  559.0 2.4 copy-start.25
  559.0 2.4 copy-start.26
  559.0 2.4 copy-start.27
  559.0 2.4 copy-start.28
  559.0 2.4 copy-start.29
  559.0 2.4 copy-start.30
  559.0 2.4 copy-start.31
  559.1 2.4 copy-start.32
  559.1 2.4 copy-start.33
  559.1 2.4 copy-start.34
  559.1 2.4 copy-start.35
  559.1 2.4 copy-start.36
  (17 other events, 12.9 us)
